TPU v7x, 128 devices: a whole 4x4x4 slice. The times are simulated.
128 devices in a mesh: tri: 2 (over x_hi), blk: 64 (over y, x_lo, z, core).
Axes of the slice: x: 4 (x_hi: 2, x_lo: 2; x = x_hi * 2 + x_lo), y: 4, z: 4, core: 2. Of those that a mesh axis runs over, the one named last changes fastest.
Arguments:
- layers: float32 [384, 4, 393216], P(('tri', 'blk')), as said below
- tile_mask: int32 [384, 1, 24], P(('tri', 'blk')), may hold values 0 or 1
- depth_order: int32 [384], replicated, may hold values from 0 to 383, as said below
Outputs:
- composite: float32 [4, 393216], P(None, 'blk')
Inputs may be any that keep to these rules, and one draw needn't show every extreme that they name: `layers`: in each rank's layer the first three channels lie between 0 and channel 3, and channel 3 lies between 0 and 6 / 384. `depth_order`: A permutation. Ranks are numbered so that device d of the mesh (tri index times 64 plus blk index) holds ranks 3 * d to 3 * d + 2, and these take consecutive positions. The 64 devices of one tri index hold consecutive positions, and for every bit b, the devices of one tri index that agree on all bits of the blk index above bit b hold consecutive positions.
All inputs are finite; a program needn't handle non-finite values. No bound on the sum of `tile_mask` on one device may be relied on, other than what follows from the above.
Results may differ from a plain program's by a relative error of at most 0.00002.
Values sent between devices are 32-bit elements; how exact they have to be, the bound alone decides.
A program may use at most 128 MiB of HBM per device.

v0:
```python
import jax
import jax.numpy as jnp
from jax import lax
from jax.sharding import PartitionSpec as P

WIDTH = 3072
TILE = 128


def blend_pair(nearer, farther):
    return nearer + (1.0 - nearer[3:4]) * farther


def blend_ordered(ordered):
    while ordered.shape[1] > 1:
        paired = ordered.reshape(4, ordered.shape[1] // 2, 2, ordered.shape[2])
        ordered = blend_pair(paired[:, :, 0], paired[:, :, 1])
    return ordered[:, 0]


def blend_group(stacked, depths):
    members = stacked.shape[1]
    summed = jnp.zeros_like(stacked[:, 0])
    for source in range(members):
        through = jnp.ones_like(stacked[3, 0])
        for other in range(members):
            if other != source:
                through = through * jnp.where(
                    depths[other] < depths[source], 1.0 - stacked[3, other], 1.0
                )
        summed = summed + through[None] * stacked[:, source]
    return summed


def on_device(layers, tile_mask, depth_order):
    blk_count = lax.axis_size("blk")
    tri_count = lax.axis_size("tri")
    blk_index = lax.axis_index("blk")
    tri_index = lax.axis_index("tri")
    device_index = tri_index * blk_count + blk_index
    rank_dev = layers.shape[0]
    pixels = layers.shape[2]
    tile_rows = pixels // WIDTH // TILE
    tile_on = tile_mask.astype(jnp.float32)
    masked = (
        layers.reshape(rank_dev, 4, tile_rows, TILE, WIDTH // TILE, TILE)
        * tile_on[:, None, :, None, :, None]
    )
    masked = masked.reshape(rank_dev, 4, pixels)
    own_depths = lax.dynamic_slice_in_dim(depth_order, device_index * rank_dev, rank_dev)
    local_image = blend_group(jnp.moveaxis(masked, 0, 1), own_depths)
    device_depth = jnp.min(depth_order.reshape(-1, rank_dev), axis=1)
    partial_value = local_image.reshape(4, blk_count, pixels // blk_count)
    received = lax.all_to_all(partial_value, "blk", split_axis=1, concat_axis=1, tiled=True)
    group_depths = lax.dynamic_slice_in_dim(device_depth, tri_index * blk_count, blk_count)
    position = (group_depths - jnp.min(group_depths)) // rank_dev
    inverse = (
        jnp.zeros((blk_count,), jnp.int32).at[position].set(jnp.arange(blk_count, dtype=jnp.int32))
    )
    ordered = jnp.take(received, inverse, axis=1)
    own_block = blend_ordered(ordered)
    group_devices = jnp.arange(tri_count, dtype=jnp.int32) * blk_count + blk_index
    tri_depths = device_depth[group_devices]
    gathered = lax.all_gather(own_block[:, None, :], "tri", axis=1, tiled=True)
    composite = blend_group(gathered, tri_depths)
    return composite


def solution(mesh):
    in_specs = (P(("tri", "blk"), None, None), P(("tri", "blk"), None, None), P())
    out_specs = P(None, "blk")
    return jax.shard_map(
        on_device, mesh=mesh, in_specs=in_specs, out_specs=out_specs, check_vma=False
    )
```

profile of v0, /device:TPU:32, one launch (start us, length us, event | category | flops | bytes accessed | tf_op | source)
XLA Modules:
  0.0 227.3 jit_solution(562508941444263034)
XLA Ops:
  0.0 0.8 dynamic_slice.7
  0.8 0.6 fusion.29
  8.9 0.7 convert_element_type.3
  9.6 0.4 mul.178
  10.0 14.3 %copy.26 = f32[1,3,3072,128]{3,1,2,0:T(4,128)} copy(f32[1,3,3072,128]{3,2,1,0:T(8,128)S(1)} %bitcast.97) | data formatting | bytes 9437184
  24.3 19.1 %multiply_bitcast_fusion = f32[4,3,393216]{2,0,1:T(4,128)} fusion(f32[3,4,393216]{2,1,0:T(4,128)} %param.3, f32[3,393216]{1,0:T(4,128)} %bitcast.96), kind=kLoop, calls=%fused_computation.3 | loop fusion | flops 4718592 | bytes 42467328 | tf_op jit(solution)/shard_map/transpose | solution.py:51
  43.4 13.8 %fusion.23 = (f32[4,1,393216]{2,0,1:T(4,128)}, f32[4,1,393216]{2,0,1:T(4,128)}, f32[4,1,393216]{2,0,1:T(4,128)}) fusion(f32[4,3,393216]{2,0,1:T(4,128)} %multiply_bitcast_fusion), kind=kLoop, calls=%fused_computation.69 | loop fusion | bytes 37748736 | tf_op jit(solution)/shard_map/slice | solution.py:31
  57.3 22.5 %fusion.1 = (f32[393216]{0:T(1024)S(1)}, f32[393216]{0:T(1024)}, f32[393216]{0:T(1024)}) fusion(pred[]{:T(512)} %bitcast.2, pred[]{:T(512)} %bitcast.4, f32[4,3,393216]{2,0,1:T(4,128)} %multiply_bitcast_fusion, pred[]{:T(512)} %bitcast.10, pred[]{:T(512)} %bitcast.9, pred[]{:T(512)} %bitcast.7, pred[]{:T(512)} %bitcast.6), kind=kLoop, calls=%fused_computation.15 | loop fusion | flops 4718592 | bytes 9437190 | tf_op jit(solution)/shard_map/mul | solution.py:28
  79.9 1.6 mul.187
  81.5 2.6 %mul.191 = f32[64,6144]{1,0:T(8,128)} reshape(f32[393216]{0:T(1024)} %get-tuple-element.6) | data formatting | bytes 3145728 | tf_op jit(solution)/shard_map/mul | solution.py:28
  84.1 12.7 %multiply_add_fusion = f32[4,64,6144]{2,0,1:T(4,128)} fusion(f32[4,64,6144]{2,0,1:T(4,128)} %bitcast.93, f32[4,64,6144]{2,0,1:T(4,128)} %bitcast.94, f32[4,64,6144]{2,0,1:T(4,128)} %bitcast.92, f32[64,6144]{1,0:T(8,128)} %mul.191, f32[64,6144]{1,0:T(8,128)S(1)} %mul.187, f32[64,6144]{1,0:T(8,128)S(1)} %mul.183), kind=kLoop, calls=%fused_computation.6 | loop fusion | flops 7864320 | bytes 29884416 | tf_op jit(solution)/shard_map/add | solution.py:31
  96.8 9.8 %all-to-all-start = ((f32[4,64,6144]{2,0,1:T(4,128)}), f32[4,64,6144]{2,0,1:T(4,128)}, u32[]{:S(2)}, u32[]{:S(2)}) async-start(f32[4,64,6144]{2,0,1:T(4,128)} %multiply_add_fusion), calls=%async_computation | async-start | bytes 12582912 | tf_op jit(solution)/shard_map/all_to_all | solution.py:54
  107.0 0.6 gather_fusion
  107.6 0.6 fusion.28
  110.8 0.7 dynamic-slice_reduce_fusion
  111.5 0.7 compare_select_fusion.1
  112.2 0.8 scatter_custom_fusion
  113.2 75.1 %all-to-all-done = f32[4,64,6144]{2,0,1:T(4,128)} async-done(((f32[4,64,6144]{2,0,1:T(4,128)}), f32[4,64,6144]{2,0,1:T(4,128)}, u32[]{:S(2)}, u32[]{:S(2)}) %all-to-all-start) | async-done | bytes 6291488 | tf_op jit(solution)/shard_map/all_to_all | solution.py:54
  188.4 9.4 %gather_fusion.1 = f32[64,4,6144]{2,1,0:T(4,128)} fusion(f32[4,64,6144]{2,0,1:T(4,128)} %all-to-all-done, s32[1024]{0:T(1024)S(1)} %pad_clamp_fusion), kind=kCustom, calls=%fused_computation.1 | custom fusion | bytes 12583168 | tf_op jit(solution)/shard_map/jit(_take)/gather | solution.py:60
  197.7 4.5 %copy_select_fusion = f32[4,32,2,6144]{3,0,1,2:T(4,128)S(1)} fusion(f32[4,32,2,6144]{3,0,2,1:T(4,128)} %bitcast.95, pred[32,2]{0,1:T(4,128)(4,1)S(1)} %copy.11), kind=kLoop, calls=%fused_computation.5 | loop fusion | flops 1572864 | bytes 12582976 | tf_op jit(solution)/shard_map/jit(_take)/select_n | solution.py:60
  202.2 2.1 fusion.24
  204.3 3.3 %fusion.7 = f32[32,6144]{1,0:T(8,128)} fusion(f32[4,32,2,6144]{3,0,1,2:T(4,128)S(1)} %copy_select_fusion), kind=kLoop, calls=%fused_computation.26 | loop fusion | flops 196608 | bytes 1572864 | tf_op jit(solution)/shard_map/sub | solution.py:11
  207.6 2.5 %sub.154 = f32[16,2,6144]{2,1,0:T(2,128)} reshape(f32[32,6144]{1,0:T(8,128)} %fusion.7) | data formatting | bytes 1572864 | tf_op jit(solution)/shard_map/sub | solution.py:11
  210.1 3.3 %multiply_add_fusion.1 = f32[4,16,2,6144]{3,0,2,1:T(4,128)S(1)} fusion(f32[4,16,2,6144]{3,0,2,1:T(4,128)} %bitcast.99, f32[4,16,2,6144]{3,0,2,1:T(4,128)S(1)} %bitcast.98, f32[16,2,6144]{2,1,0:T(2,128)} %sub.154), kind=kLoop, calls=%fused_computation.7 | loop fusion | flops 1572864 | bytes 10223616 | tf_op jit(solution)/shard_map/add | solution.py:11
  213.6 1.9 fusion.9
  215.6 1.2 sub.157
  216.8 0.9 fusion.6
  217.8 0.6 fusion.13
  218.5 0.3 fusion.8
  218.9 0.3 fusion.19
  219.7 6.8 %all_gather.3 = f32[4,2,6144]{2,0,1:T(4,128)S(1)} all-gather(f32[4,1,6144]{2,0,1:T(4,128)S(1)} %fusion.18), channel_id=1, replica_groups=mesh['tri'=2,'blk'=64] {'tri'}, dimensions={1}, use_global_device_ids=true | all-gather | bytes 294912 | tf_op jit(solution)/shard_map/all_gather | solution.py:64
  226.6 0.7 fusion.15
  (26 shorter events, 1.9 us)
Async XLA Ops:
  96.8 9.8 %copy-start = (s32[384]{0:T(512)S(1)}, s32[384]{0:T(512)}, u32[]{:S(2)}) copy-start(s32[384]{0:T(512)} %param.5) | copy-start | bytes 4612
  96.8 91.6 %all-to-all-start = ((f32[4,64,6144]{2,0,1:T(4,128)}), f32[4,64,6144]{2,0,1:T(4,128)}, u32[]{:S(2)}, u32[]{:S(2)}) async-start(f32[4,64,6144]{2,0,1:T(4,128)} %multiply_add_fusion), calls=%async_computation | async-start | bytes 12582912 | tf_op jit(solution)/shard_map/all_to_all | solution.py:54
where the time goes:
time: 228 us; the launch traced here: 227 us
  waiting for transfers between devices  75.1 us (33%)
  other arithmetic  72.7 us (32%)
  local copies, waits for them, and re-layouts  52.4 us (23%)
  between operations  10.4 us (5%)
  starting transfers between devices  9.83 us (4%)
  blocking collectives  6.79 us (3%)
    all_to_all x1, waiting for transfers between devices, on_device(): lax.all_to_all(partial_value, 'blk', split_axis=1, concat_axis=1, tiled=T...  75.1 us
    mul x1, other arithmetic, blend_group(): through * jnp.where(depths[other] < depths[source], 1.0 - stacked[3, othe...  22.5 us
    transpose x1, other arithmetic, on_device(): local_image = blend_group(jnp.moveaxis(masked, 0, 1), own_depths)  19.1 us
    unnamed x5, local copies, waits for them, and re-layouts  14.4 us
    slice x1, local copies, waits for them, and re-layouts, blend_group(): summed = summed + through[None] * stacked[:, source]  13.8 us
    add x2, other arithmetic, blend_group(): summed = summed + through[None] * stacked[:, source]  13.4 us
    all_to_all x1, starting transfers between devices, on_device(): lax.all_to_all(partial_value, 'blk', split_axis=1, concat_axis=1, tiled=T...  9.83 us
    gather x1, local copies, waits for them, and re-layouts, on_device(): ordered = jnp.take(received, inverse, axis=1)  9.36 us
  transfers between devices with their start and end apart: 1, of which 1 were waited for; matrix products, arithmetic and copies ran while one was open for 2% of the time, Pallas kernels for 0%

commit v1 on v0

--- a/solution.py
+++ b/solution.py
@@ -61,7 +61,11 @@
     own_block = blend_ordered(ordered)
     group_devices = jnp.arange(tri_count, dtype=jnp.int32) * blk_count + blk_index
     tri_depths = device_depth[group_devices]
-    gathered = lax.all_gather(own_block[:, None, :], "tri", axis=1, tiled=True)
+    block = own_block[:, None, :]
+    size = lax.axis_size("tri")
+    blocks = jnp.stack([block for _ in range(size)])
+    blocks = lax.all_to_all(blocks, "tri", split_axis=0, concat_axis=0)
+    gathered = jnp.concatenate(blocks, axis=1)
     composite = blend_group(gathered, tri_depths)
     return composite
 

time: 228 us -> 232 us (1.018)
  blocking collectives: 6.79 us -> 0 us
  waiting for transfers between devices: 75.1 us -> 81.6 us
  starting transfers between devices: 9.83 us -> 13.8 us
    all_gather x1 -> x0, blocking collectives: 6.79 us -> none  [on_device(): gathered = lax.all_gather(own_block[:, None, :], 'tri', axis=1, tiled=True)]
    all_to_all x0 -> x1, starting transfers between devices: none -> 4 us  [on_device(): blocks = lax.all_to_all(blocks, 'tri', split_axis=0, concat_axis=0)]
    all_to_all x0 -> x1, waiting for transfers between devices: none -> 3.33 us  [on_device(): blocks = lax.all_to_all(blocks, 'tri', split_axis=0, concat_axis=0)]
    all_to_all x1, waiting for transfers between devices: 75.1 us -> 78.3 us  [on_device(): lax.all_to_all(partial_value, 'blk', split_axis=1, concat_axis=1, tiled=T...]
  transfers between devices with their start and end apart: 1 -> 2, of which waited for: 1 -> 2; matrix products, arithmetic and copies ran while one was open for 2% -> 2% of each run, Pallas kernels for 0% -> 0%
where the time goes in v1:
time: 232 us
  waiting for transfers between devices  81.6 us (35%)
  other arithmetic  73.4 us (32%)
  local copies, waits for them, and re-layouts  52.4 us (23%)
  starting transfers between devices  13.8 us (6%)
  between operations  10.2 us (4%)
    all_to_all x1, waiting for transfers between devices, on_device(): lax.all_to_all(partial_value, 'blk', split_axis=1, concat_axis=1, tiled=T...  78.3 us
    mul x1, other arithmetic, blend_group(): through * jnp.where(depths[other] < depths[source], 1.0 - stacked[3, othe...  22.5 us
    transpose x1, other arithmetic, on_device(): local_image = blend_group(jnp.moveaxis(masked, 0, 1), own_depths)  19.1 us
    unnamed x5, local copies, waits for them, and re-layouts  14.4 us
    slice x1, local copies, waits for them, and re-layouts, blend_group(): summed = summed + through[None] * stacked[:, source]  13.8 us
    add x2, other arithmetic, blend_group(): summed = summed + through[None] * stacked[:, source]  13.4 us
    all_to_all x1, starting transfers between devices, on_device(): lax.all_to_all(partial_value, 'blk', split_axis=1, concat_axis=1, tiled=T...  9.83 us
    gather x1, local copies, waits for them, and re-layouts, on_device(): ordered = jnp.take(received, inverse, axis=1)  9.36 us
  transfers between devices with their start and end apart: 2, of which 2 were waited for; matrix products, arithmetic and copies ran while one was open for 2% of the time, Pallas kernels for 0%

profile of v1, /device:TPU:32, one launch (start us, length us, event | category | flops | bytes accessed | tf_op | source)
XLA Modules:
  0.0 231.5 jit_solution(3422038413661824106)
XLA Ops:
  0.0 0.8 dynamic_slice.7
  0.8 0.6 fusion.29
  8.9 0.7 convert_element_type.3
  9.6 0.4 mul.179
  10.0 14.3 %copy.24 = f32[1,3,3072,128]{3,1,2,0:T(4,128)} copy(f32[1,3,3072,128]{3,2,1,0:T(8,128)S(1)} %bitcast.100) | data formatting | bytes 9437184
  24.3 19.1 %multiply_bitcast_fusion = f32[4,3,393216]{2,0,1:T(4,128)} fusion(f32[3,4,393216]{2,1,0:T(4,128)} %param.3, f32[3,393216]{1,0:T(4,128)} %bitcast.99), kind=kLoop, calls=%fused_computation.3 | loop fusion | flops 4718592 | bytes 42467328 | tf_op jit(solution)/shard_map/transpose | solution.py:51
  43.4 13.8 %fusion.23 = (f32[4,1,393216]{2,0,1:T(4,128)}, f32[4,1,393216]{2,0,1:T(4,128)}, f32[4,1,393216]{2,0,1:T(4,128)}) fusion(f32[4,3,393216]{2,0,1:T(4,128)} %multiply_bitcast_fusion), kind=kLoop, calls=%fused_computation.70 | loop fusion | bytes 37748736 | tf_op jit(solution)/shard_map/slice | solution.py:31
  57.3 22.5 %fusion.1 = (f32[393216]{0:T(1024)S(1)}, f32[393216]{0:T(1024)}, f32[393216]{0:T(1024)}) fusion(pred[]{:T(512)} %bitcast.2, pred[]{:T(512)} %bitcast.4, f32[4,3,393216]{2,0,1:T(4,128)} %multiply_bitcast_fusion, pred[]{:T(512)} %bitcast.10, pred[]{:T(512)} %bitcast.9, pred[]{:T(512)} %bitcast.7, pred[]{:T(512)} %bitcast.6), kind=kLoop, calls=%fused_computation.15 | loop fusion | flops 4718592 | bytes 9437190 | tf_op jit(solution)/shard_map/mul | solution.py:28
  79.9 1.6 mul.188
  81.5 2.6 %mul.192 = f32[64,6144]{1,0:T(8,128)} reshape(f32[393216]{0:T(1024)} %get-tuple-element.6) | data formatting | bytes 3145728 | tf_op jit(solution)/shard_map/mul | solution.py:28
  84.1 12.7 %multiply_add_fusion = f32[4,64,6144]{2,0,1:T(4,128)} fusion(f32[4,64,6144]{2,0,1:T(4,128)} %bitcast.96, f32[4,64,6144]{2,0,1:T(4,128)} %bitcast.97, f32[4,64,6144]{2,0,1:T(4,128)} %bitcast.95, f32[64,6144]{1,0:T(8,128)} %mul.192, f32[64,6144]{1,0:T(8,128)S(1)} %mul.188, f32[64,6144]{1,0:T(8,128)S(1)} %mul.184), kind=kLoop, calls=%fused_computation.6 | loop fusion | flops 7864320 | bytes 29884416 | tf_op jit(solution)/shard_map/add | solution.py:31
  96.8 9.8 %all-to-all-start = ((f32[4,64,6144]{2,0,1:T(4,128)}), f32[4,64,6144]{2,0,1:T(4,128)}, u32[]{:S(2)}, u32[]{:S(2)}) async-start(f32[4,64,6144]{2,0,1:T(4,128)} %multiply_add_fusion), calls=%async_computation | async-start | bytes 12582912 | tf_op jit(solution)/shard_map/all_to_all | solution.py:54
  107.0 0.7 dynamic-slice_reduce_fusion
  107.7 0.7 compare_select_fusion.1
  108.4 0.8 scatter_custom_fusion
  109.5 0.6 gather_fusion
  110.1 78.3 %all-to-all-done = f32[4,64,6144]{2,0,1:T(4,128)} async-done(((f32[4,64,6144]{2,0,1:T(4,128)}), f32[4,64,6144]{2,0,1:T(4,128)}, u32[]{:S(2)}, u32[]{:S(2)}) %all-to-all-start) | async-done | bytes 6291488 | tf_op jit(solution)/shard_map/all_to_all | solution.py:54
  188.4 9.4 %gather_fusion.1 = f32[64,4,6144]{2,1,0:T(4,128)} fusion(f32[4,64,6144]{2,0,1:T(4,128)} %all-to-all-done, s32[1024]{0:T(1024)S(1)} %pad_clamp_fusion), kind=kCustom, calls=%fused_computation.1 | custom fusion | bytes 12583168 | tf_op jit(solution)/shard_map/jit(_take)/gather | solution.py:60
  197.7 4.5 %copy_select_fusion = f32[4,32,2,6144]{3,0,1,2:T(4,128)S(1)} fusion(f32[4,32,2,6144]{3,0,2,1:T(4,128)} %bitcast.98, pred[32,2]{0,1:T(4,128)(4,1)S(1)} %copy.9), kind=kLoop, calls=%fused_computation.5 | loop fusion | flops 1572864 | bytes 12582976 | tf_op jit(solution)/shard_map/jit(_take)/select_n | solution.py:60
  202.2 2.1 fusion.24
  204.3 3.3 %fusion.7 = f32[32,6144]{1,0:T(8,128)} fusion(f32[4,32,2,6144]{3,0,1,2:T(4,128)S(1)} %copy_select_fusion), kind=kLoop, calls=%fused_computation.26 | loop fusion | flops 196608 | bytes 1572864 | tf_op jit(solution)/shard_map/sub | solution.py:11
  207.6 2.5 %sub.154 = f32[16,2,6144]{2,1,0:T(2,128)} reshape(f32[32,6144]{1,0:T(8,128)} %fusion.7) | data formatting | bytes 1572864 | tf_op jit(solution)/shard_map/sub | solution.py:11
  210.1 3.3 %multiply_add_fusion.1 = f32[4,16,2,6144]{3,0,2,1:T(4,128)S(1)} fusion(f32[4,16,2,6144]{3,0,2,1:T(4,128)} %bitcast.102, f32[4,16,2,6144]{3,0,2,1:T(4,128)S(1)} %bitcast.101, f32[16,2,6144]{2,1,0:T(2,128)} %sub.154), kind=kLoop, calls=%fused_computation.7 | loop fusion | flops 1572864 | bytes 10223616 | tf_op jit(solution)/shard_map/add | solution.py:11
  213.6 1.9 fusion.9
  215.6 1.2 sub.157
  216.8 0.9 fusion.6
  217.8 0.6 fusion.13
  219.7 0.7 pad_maximum_fusion
  220.4 4.0 %all-to-all-start.1 = ((f32[2,4,1,6144]{3,1,2,0:T(4,128)}), f32[2,4,1,6144]{3,1,2,0:T(4,128)S(1)}, u32[]{:S(2)}, u32[]{:S(2)}) async-start(f32[2,4,1,6144]{3,1,2,0:T(4,128)} %pad_maximum_fusion), calls=%async_computation.1 | async-start | bytes 393216 | tf_op jit(solution)/shard_map/all_to_all | solution.py:67
  224.4 0.6 fusion.28
  227.4 3.3 %all-to-all-done.1 = f32[2,4,1,6144]{3,1,2,0:T(4,128)S(1)} async-done(((f32[2,4,1,6144]{3,1,2,0:T(4,128)}), f32[2,4,1,6144]{3,1,2,0:T(4,128)S(1)}, u32[]{:S(2)}, u32[]{:S(2)}) %all-to-all-start.1) | async-done | bytes 196640 | tf_op jit(solution)/shard_map/all_to_all | solution.py:67
  230.8 0.7 fusion.15
  (28 shorter events, 2.5 us)
Async XLA Ops:
  96.8 9.8 %copy-start = (s32[384]{0:T(512)S(1)}, s32[384]{0:T(512)}, u32[]{:S(2)}) copy-start(s32[384]{0:T(512)} %param.5) | copy-start | bytes 4612
  96.8 91.6 %all-to-all-start = ((f32[4,64,6144]{2,0,1:T(4,128)}), f32[4,64,6144]{2,0,1:T(4,128)}, u32[]{:S(2)}, u32[]{:S(2)}) async-start(f32[4,64,6144]{2,0,1:T(4,128)} %multiply_add_fusion), calls=%async_computation | async-start | bytes 12582912 | tf_op jit(solution)/shard_map/all_to_all | solution.py:54
  220.4 10.3 %all-to-all-start.1 = ((f32[2,4,1,6144]{3,1,2,0:T(4,128)}), f32[2,4,1,6144]{3,1,2,0:T(4,128)S(1)}, u32[]{:S(2)}, u32[]{:S(2)}) async-start(f32[2,4,1,6144]{3,1,2,0:T(4,128)} %pad_maximum_fusion), calls=%async_computation.1 | async-start | bytes 393216 | tf_op jit(solution)/shard_map/all_to_all | solution.py:67
